TPU v7x, 32 devices: a whole 2x2x4 slice. The times are simulated.
32 devices in a mesh: vis: 8 (over z, x), tile: 4 (over y, core).
Axes of the slice: x: 2, y: 2, z: 4, core: 2. Of those that a mesh axis runs over, the one named last changes fastest.
Arguments:
- spectra: bfloat16 [64, 2048], P(None, ('vis', 'tile')), may hold values from -0.1875 to 0.1875
- positions: int32 [2, 2048], P(None, ('vis', 'tile')), may hold values from 0 to 8191
- observed: bfloat16 [32768, 128], P(('vis', 'tile')), may hold values from -6 to 6
- cells: int32 [2, 32768], P(None, ('vis', 'tile')), may hold values from 0 to 8184, as said below
- fractions: float32 [2, 32768], P(None, ('vis', 'tile')), may hold values from 0 to 1
- bucket_counts: int32 [32, 4], P(('vis', 'tile')), may hold values from 0 to 512, as said below
- chan_weights: float32 [64], replicated, may hold values from 0.04 to 0.32
Outputs:
- residual_vis: bfloat16 [32768, 128], P(('vis', 'tile'))
- residual_grid: float32 [128, 2, 8192], P('vis', None, 'tile')
Inputs may be any that keep to these rules, and one draw needn't show every extreme that they name: cells[0, r] is the first uv column and cells[1, r] the first uv row of row r's 8 x 8 kernel window, with cells[1, r] <= 120. The rows of each device are ordered by tile: for device d and tile t, the bucket_counts[d, t] rows that start after the first sum of bucket_counts[d, 0:t] rows have cells[0] between t * 2048 and (t + 1) * 2048 - 8; rows after a device's total are unused. `bucket_counts`: each device's counts sum to at most 1024. For every index of vis, one tile receives exactly 512 rows from every device with that vis index; which tile is drawn.
All inputs are finite; a program needn't handle non-finite values.
Results may differ from a plain program's by a relative error of at most 0.008.
Values may be sent and summed in bfloat16 or wider, within the bound.
A program may use at most 64 MiB of HBM per device.

v0:
```python
import math

import jax
import jax.numpy as jnp
from jax import lax
from jax.sharding import PartitionSpec as P

GRID = 8192
BAND = 128
TAPS = 8


def predict_piece(running, shard_part, first_col, first_row, col_frac, row_frac):
    spec_piece, pos_piece = shard_part
    col_pixel = pos_piece[0]
    row_pixel = pos_piece[1]
    turn_count = jnp.mod(
        (first_col + 3)[:, None] * col_pixel[None, :]
        + (first_row + 3)[:, None] * row_pixel[None, :],
        GRID,
    )
    phase_turns = (
        turn_count.astype(jnp.float32)
        + col_frac[:, None] * col_pixel.astype(jnp.float32)[None, :]
        + row_frac[:, None] * row_pixel.astype(jnp.float32)[None, :]
    )
    angles = phase_turns * (2.0 * math.pi / GRID)
    cosine = jnp.cos(angles).astype(jnp.bfloat16)
    sine_table = jnp.sin(angles).astype(jnp.bfloat16)
    contract_dims = (((1,), (1,)), ((), ()))
    real_part = lax.dot_general(
        cosine, spec_piece, contract_dims, preferred_element_type=jnp.float32
    )
    imag_part = lax.dot_general(
        sine_table, spec_piece, contract_dims, preferred_element_type=jnp.float32
    )
    return (real_part, running[1] - imag_part)


def kernel_weights(offsets):
    taps_float = jnp.arange(TAPS, dtype=jnp.int32).astype(jnp.float32)
    shifted = taps_float[None, :] - 3.0 - offsets[:, None]
    return jnp.exp(-0.5 * (shifted * shifted))


def place_taps(offset, tap_table):
    placed = jnp.zeros(offset.shape, jnp.float32)
    for tap_number in range(TAPS):
        placed = jnp.where(offset == tap_number, tap_table[:, tap_number : tap_number + 1], placed)
    return placed


def spread_rows(first_col, col_frac, col_base, tile_width):
    offset = jnp.arange(tile_width, dtype=jnp.int32)[None, :] - (first_col - col_base)[:, None]
    return place_taps(offset, kernel_weights(col_frac)).astype(jnp.bfloat16)


def left_rows(values, first_row, row_frac, band_count):
    offset = jnp.arange(band_count, dtype=jnp.int32)[None, :] - first_row[:, None]
    weight = place_taps(offset, kernel_weights(row_frac))
    return (values[:, :, None] * weight[None, :, :]).astype(jnp.bfloat16)


def accumulate(spread, values, first_row, row_frac, group_total, band_count):
    slot_total = spread.shape[0]
    tile_width = spread.shape[1]
    group_size = slot_total // group_total
    block_rows = min(256, group_size)
    per_group = group_size // block_rows
    block_total = slot_total // block_rows
    spread_blocks = spread.reshape(block_total, block_rows, tile_width)
    value_blocks = values.reshape(2, block_total, block_rows).transpose(1, 0, 2)
    row_blocks = first_row.reshape(block_total, block_rows)
    frac_blocks = row_frac.reshape(block_total, block_rows)
    group_of = jnp.arange(block_total, dtype=jnp.int32) // per_group

    def block_term(block_data):
        left_table = left_rows(block_data[1], block_data[2], block_data[3], band_count)
        return jnp.einsum(
            "cbv,bu->vcu", left_table, block_data[0], preferred_element_type=jnp.float32
        )

    def scan_step(totals, block_data):
        totals = totals + block_term(block_data)
        return (totals, None)

    start_totals = jnp.zeros((band_count, 2, tile_width), jnp.float32)
    finished, unused = lax.scan(
        scan_step, start_totals, (spread_blocks, value_blocks, row_blocks, frac_blocks, group_of)
    )
    return finished


def on_device(spectra, positions, observed, cells, fractions, bucket_counts, chan_weights):
    row_count = observed.shape[0]
    channels = observed.shape[1] // 2
    tile_count = lax.axis_size("tile")
    tile_width = GRID // tile_count
    slot_size = row_count // 2
    band_rows = BAND // lax.axis_size("vis")
    first_col = cells[0]
    first_row = cells[1]
    col_frac = fractions[0]
    row_frac = fractions[1]
    bucket_sizes = bucket_counts[0]
    zeros_init = jnp.zeros((row_count, channels), jnp.float32)
    real_part, imag_part = predict_piece(
        (zeros_init, zeros_init),
        (
            lax.all_gather(spectra, ("vis", "tile"), axis=1, tiled=True),
            lax.all_gather(positions, ("vis", "tile"), axis=1, tiled=True),
        ),
        first_col,
        first_row,
        col_frac,
        row_frac,
    )
    predicted = jnp.concatenate([real_part, imag_part], axis=1)
    row_live = jnp.arange(row_count, dtype=jnp.int32) < jnp.sum(bucket_sizes)
    residual = jnp.where(row_live[:, None], observed.astype(jnp.float32) - predicted, 0.0).astype(
        jnp.bfloat16
    )
    widened = residual.astype(jnp.float32)
    value_real = jnp.sum(widened[:, :channels] * chan_weights[None, :], axis=1)
    value_imag = jnp.sum(widened[:, channels:] * chan_weights[None, :], axis=1)
    bucket_start = jnp.cumsum(bucket_sizes) - bucket_sizes
    slot_index = bucket_start[:, None] + jnp.arange(slot_size, dtype=jnp.int32)[None, :]
    slot_live = jnp.arange(slot_size, dtype=jnp.int32)[None, :] < bucket_sizes[:, None]
    float_rows = jnp.pad(
        jnp.stack([value_real, value_imag, col_frac, row_frac]), ((0, 0), (0, slot_size))
    )
    cell_rows = jnp.pad(cells, ((0, 0), (0, slot_size)))
    gathered = jnp.take(float_rows, slot_index, axis=1).transpose(1, 0, 2)
    packed_values = jnp.concatenate(
        [jnp.where(slot_live[:, None, :], gathered[:, 0:2], 0.0), gathered[:, 2:]], axis=1
    )
    packed_cells = jnp.take(cell_rows, slot_index, axis=1).transpose(1, 0, 2)
    slot_total = tile_count * slot_size
    got_values, got_cells, got_sizes = (
        lax.all_to_all(packed_values, "tile", split_axis=0, concat_axis=0, tiled=True),
        lax.all_to_all(packed_cells, "tile", split_axis=0, concat_axis=0, tiled=True),
        lax.all_to_all(bucket_sizes[:, None], "tile", split_axis=0, concat_axis=0, tiled=True),
    )
    values = got_values[:, 0:2].transpose(1, 0, 2).reshape(2, slot_total)
    spread = spread_rows(
        got_cells[:, 0].reshape(slot_total),
        got_values[:, 2].reshape(slot_total),
        lax.axis_index("tile") * tile_width,
        tile_width,
    )
    owner_rows = got_cells[:, 1].reshape(slot_total)
    owner_frac = got_values[:, 3].reshape(slot_total)
    grid_share = lax.psum_scatter(
        accumulate(
            spread, values, owner_rows, owner_frac, tile_count, band_rows * lax.axis_size("vis")
        ),
        "vis",
        scatter_dimension=0,
        tiled=True,
    )
    return (residual, grid_share)


def solution(mesh):
    placed = (
        P(None, ("vis", "tile")),
        P(None, ("vis", "tile")),
        P(("vis", "tile"), None),
        P(None, ("vis", "tile")),
        P(None, ("vis", "tile")),
        P(("vis", "tile"), None),
        P(),
    )
    return jax.shard_map(
        on_device,
        mesh=mesh,
        in_specs=placed,
        out_specs=(P(("vis", "tile"), None), P("vis", None, "tile")),
        check_vma=False,
    )
```

profile of v0, /device:TPU:0, one launch (start us, length us, event | category | flops | bytes accessed | tf_op | source)
XLA Modules:
  0.0 339.4 jit_solution(17643657220523912237)
XLA Ops:
  7.2 0.9 reduce-window.8
  8.1 0.7 bitcast_subtract_fusion
  8.9 0.9 copy.28
  9.9 5.5 %gather_fusion = s32[2048,2]{1,0:T(8,128)S(1)} fusion(s32[2,1536]{0,1:T(8,128)S(1)} %pad.8, s32[2048]{0:T(1024)S(1)} %broadcast_clamp_fusion), kind=kCustom, calls=%fused_computation | custom fusion | bytes 40960 | tf_op jit(solution)/shard_map/jit(_take)/gather | solution.py:137
  16.3 4.3 %all-to-all-start = ((s32[4,2,512]{2,1,0:T(2,128)}), s32[4,2,512]{2,1,0:T(2,128)S(1)}, u32[]{:S(2)}, u32[]{:S(2)}) async-start(s32[4,2,512]{2,1,0:T(2,128)} %select_bitcast_fusion.1), calls=%async_computation | async-start | bytes 32768 | tf_op jit(solution)/shard_map/all_to_all | solution.py:141
  20.6 0.8 slice_add_fusion.1
  21.4 43.1 %all-gather = s32[32,64,2]{1,2,0:T(2,128)S(1)} all-gather(s32[1,64,2]{1,2,0:T(2,128)} %bitcast.124), channel_id=1, replica_groups=mesh['vis'=8,'tile'=4] {'vis','tile'}, dimensions={0}, use_global_device_ids=true | all-gather | bytes 16896 | tf_op jit(solution)/shard_map/all_gather | solution.py:111
  64.5 0.8 fusion.53
  65.3 35.0 %cosine_convert_fusion.4 = bf16[1024,2048]{1,0:T(8,128)(2,1)} fusion(f32[2048]{0:T(1024)S(1)} %bitcast.106, f32[1024]{0:T(1024)S(1)} %bitcast.118, f32[2048]{0:T(1024)S(1)} %bitcast.104, f32[1024]{0:T(1024)S(1)} %bitcast.116, s32[2048]{0:T(1024)S(1)} %bitcast.108, s32[1024]{0:T(1024)S(1)} %bitcast.114, s32[2048]{0:T(1024)S(1)} %bitcast.102, ...), kind=kLoop, calls=%fused_computation.45.clone.clone.1 | loop fusion | flops 44040192 | bytes 4243456 | tf_op jit(solution)/shard_map/dot_general | solution.py:31
  100.3 35.4 %sine_convert_fusion.6 = bf16[1024,2048]{1,0:T(8,128)(2,1)} fusion(f32[2048]{0:T(1024)S(1)} %bitcast.107, f32[1024]{0:T(1024)S(1)} %bitcast.119, f32[2048]{0:T(1024)S(1)} %bitcast.105, f32[1024]{0:T(1024)S(1)} %bitcast.117, s32[2048]{0:T(1024)S(1)} %bitcast.109, s32[1024]{0:T(1024)S(1)} %bitcast.115, s32[2048]{0:T(1024)S(1)} %bitcast.103, ...), kind=kLoop, calls=%fused_computation.44.clone.clone.clone.clone.1 | loop fusion | flops 44040192 | bytes 4243456 | tf_op jit(solution)/shard_map/dot_general | solution.py:34
  135.8 0.6 reduce_sum.27
  136.5 38.2 %all_gather.7 = bf16[64,2048]{0,1:T(8,128)(2,1)S(1)} all-gather(bf16[64,64]{0,1:T(8,128)(2,1)S(1)} %copy.27), channel_id=1, replica_groups=mesh['vis'=8,'tile'=4] {'vis','tile'}, dimensions={1}, use_global_device_ids=true | all-gather | bytes 270336 | tf_op jit(solution)/shard_map/all_gather | solution.py:110
  174.8 3.6 %fusion.27 = f32[1024,64]{0,1:T(8,128)S(1)} fusion(bf16[64,2048]{0,1:T(8,128)(2,1)S(1)} %all_gather.7, bf16[1024,2048]{1,0:T(8,128)(2,1)} %cosine_convert_fusion.4), kind=kOutput, calls=%fused_computation.46 | convolution fusion | flops 268435456 | bytes 4718592 | tf_op jit(solution)/shard_map/dot_general | solution.py:31
  178.3 3.6 %fusion.31 = f32[1024,64]{0,1:T(8,128)S(1)} fusion(bf16[64,2048]{0,1:T(8,128)(2,1)S(1)} %all_gather.7, bf16[1024,2048]{1,0:T(8,128)(2,1)} %sine_convert_fusion.6), kind=kOutput, calls=%fused_computation.48 | convolution fusion | flops 268500992 | bytes 4718592 | tf_op jit(solution)/shard_map/dot_general | solution.py:34
  182.1 0.7 iota_compare_fusion.1
  183.3 5.5 %gather_fusion.1 = f32[2048,4]{1,0:T(8,128)S(1)} fusion(f32[4,1536]{0,1:T(8,128)S(1)} %pad.9, s32[2048]{0:T(1024)S(1)} %broadcast_clamp_fusion), kind=kCustom, calls=%fused_computation.1 | custom fusion | bytes 73728 | tf_op jit(solution)/shard_map/jit(_take)/gather | solution.py:133
  189.9 3.3 all-to-all-start.1
  193.3 3.8 %all-to-all-done.1 = f32[4,4,512]{2,1,0:T(4,128)S(1)} async-done(((f32[4,4,512]{2,1,0:T(4,128)}), f32[4,4,512]{2,1,0:T(4,128)S(1)}, u32[]{:S(2)}, u32[]{:S(2)}) %all-to-all-start.1) | async-done | bytes 32800 | tf_op jit(solution)/shard_map/all_to_all | solution.py:140
  197.6 11.3 %select_convert_fusion = bf16[8,256,2048]{1,2,0:T(8,128)(2,1)} fusion(bf16[8,256]{1,0:T(8,128)(2,1)S(1)} %broadcast_in_dim.215, bf16[8,256]{1,0:T(8,128)(2,1)S(1)} %broadcast_in_dim.213, bf16[8,256]{1,0:T(8,128)(2,1)S(1)} %broadcast_in_dim.211, bf16[8,256]{1,0:T(8,128)(2,1)S(1)} %broadcast_in_dim.209, bf16[8,256]{1,0:T(8,128)(2,1)S(1)} %broadcast_in_dim.207, ...), kind=kLoop, calls=%fused_computation.26 | loop fusion | flops 71303168 | bytes 8429568 | tf_op jit(solution)/shard_map/convert_element_type | solution.py:55
  208.9 21.0 %while.13 = (s32[]{:T(128)}, f32[128,2,2048]{0,2,1:T(8,128)S(1)}, bf16[8,256,2048]{1,2,0:T(8,128)(2,1)}, f32[8,2,256]{2,0,1:T(8,128)S(1)}, s32[8,256]{1,0:T(8,12...) while((s32[]{:T(128)}, f32[128,2,2048]{0,2,1:T(8,128)S(1)}, ...), condition=%wide.region_5.6_spmd.clone, body=%wide.region_4.5_spmd.clone.sunk | while | flops 270178336 | bytes 5554859 | solution.py:88
  209.5 2.1 fusion.65
  212.1 2.1 fusion.65
  214.7 2.1 fusion.65
  217.3 2.1 fusion.65
  220.0 2.1 fusion.65
  222.6 2.1 fusion.65
  225.2 2.1 fusion.65
  227.9 2.1 fusion.65
  230.0 2.4 copy.34
  232.4 0.8 copy.35
  234.5 96.4 %all-reduce.5.cloned.1.call-done = f32[128,2,2048]{2,1,0:T(2,128)} async-done(((f32[128,2,2048]{2,1,0:T(2,128)}), f32[128,2,2048]{2,1,0:T(2,128)}) %all-reduce.5.cloned.1.call-update) | async-done | bytes 2097168
  330.9 1.7 constant_dynamic-slice_fusion.3
  (122 shorter events, 8.2 us)
Async XLA Ops:
  7.2 128.6 %copy-start.4 = (s32[1,4]{1,0:T(1,128)S(1)}, s32[1,4]{1,0:T(1,128)}, u32[]{:S(2)}) copy-start(s32[1,4]{1,0:T(1,128)} %param.14) | copy-start | bytes 52
  7.2 129.2 %copy-start.2 = (bf16[64,64]{1,0:T(8,128)(2,1)S(1)}, bf16[64,64]{1,0:T(8,128)(2,1)}, u32[]{:S(2)}) copy-start(bf16[64,64]{1,0:T(8,128)(2,1)} %param.9) | copy-start | bytes 24580
  16.3 173.6 %all-to-all-start = ((s32[4,2,512]{2,1,0:T(2,128)}), s32[4,2,512]{2,1,0:T(2,128)S(1)}, u32[]{:S(2)}, u32[]{:S(2)}) async-start(s32[4,2,512]{2,1,0:T(2,128)} %select_bitcast_fusion.1), calls=%async_computation | async-start | bytes 32768 | tf_op jit(solution)/shard_map/all_to_all | solution.py:141
  100.3 81.6 %copy-start = (bf16[1024,128]{1,0:T(8,128)(2,1)S(1)}, bf16[1024,128]{1,0:T(8,128)(2,1)}, u32[]{:S(2)}) copy-start(bf16[1024,128]{1,0:T(8,128)(2,1)} %param.11) | copy-start | bytes 786436
  100.3 82.5 %copy-start.3 = (f32[64]{0:T(128)S(1)}, f32[64]{0:T(128)}, u32[]{:S(2)}) copy-start(f32[64]{0:T(128)} %param.15) | copy-start | bytes 772
  100.3 82.7 %copy-start.1 = (f32[2,1024]{1,0:T(2,128)S(1)}, f32[2,1024]{1,0:T(2,128)}, u32[]{:S(2)}) copy-start(f32[2,1024]{1,0:T(2,128)} %param.13) | copy-start | bytes 24580
  189.9 7.2 %all-to-all-start.1 = ((f32[4,4,512]{2,1,0:T(4,128)}), f32[4,4,512]{2,1,0:T(4,128)S(1)}, u32[]{:S(2)}, u32[]{:S(2)}) async-start(f32[4,4,512]{2,1,0:T(4,128)} %pad_maximum_fusion), calls=%async_computation.1 | async-start | bytes 65536 | tf_op jit(solution)/shard_map/all_to_all | solution.py:140
  193.2 137.7 %all-reduce.5.cloned.1.call-start = ((), (), s32[]{:S(2)}) async-start(), calls=%async_computation.2 | async-start | bytes 4194304
  208.9 24.3 %copy-start.5 = (u32[32]{0:T(128)S(1)}, u32[32]{0:T(128)}, u32[]{:S(2)}) copy-start(u32[32]{0:T(128)} %constant.158) | copy-start | bytes 388
Sparse Core Ops, SparseCore 0:
  232.5 98.3 all-reduce.4
where the time goes:
time: 340 us; the launch traced here: 339 us
  waiting for transfers between devices  100 us (29%)
  other arithmetic  90.9 us (27%)
  blocking collectives  81.3 us (24%)
  matrix products  23.7 us (7%)
  local copies, waits for them, and re-layouts  20.1 us (6%)
  between operations  15 us (4%)
  starting transfers between devices  7.56 us (2%)
    unnamed x2, waiting for transfers between devices  96.4 us
    all_gather x1, blocking collectives, on_device(): lax.all_gather(positions, ('vis', 'tile'), axis=1, tiled=True)  43.1 us
    all_gather x1, blocking collectives, on_device(): lax.all_gather(spectra, ('vis', 'tile'), axis=1, tiled=True)  38.2 us
    dot_general x1, other arithmetic, predict_piece(): lax.dot_general(sine_table, spec_piece, contract_dims, preferred_element_...  35.4 us
    dot_general x1, other arithmetic, predict_piece(): lax.dot_general(cosine, spec_piece, contract_dims, preferred_element_type...  35 us
    dot_general x8, matrix products, block_term(): jnp.einsum('cbv,bu->vcu', left_table, block_data[0], preferred_element_ty...  16.6 us
    convert_element_type x1, other arithmetic, spread_rows(): return place_taps(offset, kernel_weights(col_frac)).astype(jnp.bfloat16)  11.3 us
  transfers between devices with their start and end apart: 3, of which 2 were waited for; matrix products, arithmetic and copies ran while one was open for 26% of the time, Pallas kernels for 0%

commit v1 on v0

v1 whole, which is shorter than its diff:
```python
import functools
import math

import jax
import jax.numpy as jnp
from jax import lax
from jax.experimental import pallas as pl
from jax.experimental.pallas import tpu as pltpu
from jax.sharding import PartitionSpec as P

GRID = 8192
BAND = 128
TAPS = 8
MESH = pl.DeviceIdType.MESH
VMEM_LIMIT = 60 * 1024 * 1024

COS = (0.9999992107823198, -19.73898035576402, 64.92865742103395, -85.2716215343041,
       58.79049212014272, -21.071105627647917)
SIN = (-6.28305408794423, 41.33112294859376, -81.36549856606159, 74.47097754866051,
       -32.768902424225836)
EXP_SCALE = -0.5 / math.log(2.0)


def position_features(positions):
    rows = []
    for axis in range(2):
        pixel = positions[axis]
        high = (pixel + 64) >> 7
        low = pixel - 128 * high
        high_wrapped = jnp.where(high >= 32, high - 64, high)
        rows += [low] * 5 + [128 * high_wrapped] + [128 * high] * 3
    return jnp.stack(rows).astype(jnp.bfloat16)


def gather_kernel(n_vis, n_tile, block_ref, out_ref, send_sems, recv_sems, pair_sems, own_sem):
    half = n_tile // 2
    count = n_vis * half
    vis = lax.axis_index("vis")
    tile = lax.axis_index("tile")
    core = tile % 2
    mine = vis * half + tile // 2

    def peer(step):
        place = (mine + step) % count
        return {"vis": place // half, "tile": (place % half) * 2 + core}

    partner = {"vis": vis, "tile": tile + 1 - 2 * core}
    barrier = pltpu.get_barrier_semaphore()

    @pl.loop(1, count)
    def _(step):
        pl.semaphore_signal(barrier, inc=1, device_id=peer(step), device_id_type=MESH)

    pl.semaphore_signal(barrier, inc=1, device_id=partner, device_id_type=MESH)
    own = pltpu.make_async_copy(block_ref, out_ref.at[core, mine], own_sem)
    own.start()
    pl.semaphore_wait(barrier, count)

    def send(step):
        return pltpu.make_async_remote_copy(
            src_ref=block_ref,
            dst_ref=out_ref.at[core, mine],
            send_sem=send_sems.at[step],
            recv_sem=recv_sems.at[step],
            device_id=peer(step),
            device_id_type=MESH,
        )

    @pl.loop(1, count)
    def _(step):
        send(step).start()

    own.wait()

    @pl.loop(1, count)
    def _(step):
        send(step).wait_recv()

    swap = pltpu.make_async_remote_copy(
        src_ref=out_ref.at[core],
        dst_ref=out_ref.at[core],
        send_sem=pair_sems.at[0],
        recv_sem=pair_sems.at[1],
        device_id=partner,
        device_id_type=MESH,
    )
    swap.start()

    @pl.loop(1, count)
    def _(step):
        send(step).wait_send()

    swap.wait()


def gather_components(block, n_vis, n_tile):
    count = n_vis * n_tile // 2
    return pl.pallas_call(
        functools.partial(gather_kernel, n_vis, n_tile),
        out_shape=jax.ShapeDtypeStruct((2, count) + block.shape, block.dtype),
        in_specs=[pl.BlockSpec(memory_space=pltpu.VMEM)],
        out_specs=pl.BlockSpec(memory_space=pltpu.VMEM),
        scratch_shapes=[
            pltpu.SemaphoreType.DMA((count,)),
            pltpu.SemaphoreType.DMA((count,)),
            pltpu.SemaphoreType.DMA((2,)),
            pltpu.SemaphoreType.DMA,
        ],
        compiler_params=pltpu.CompilerParams(
            collective_id=0, has_side_effects=True, vmem_limit_bytes=VMEM_LIMIT
        ),
        name="gather_components",
    )(block)


def place_rows(shape, first, rows):
    place = lax.broadcasted_iota(jnp.int32, shape, 0)
    table = jnp.zeros(shape, jnp.float32)
    for index, row in enumerate(rows):
        table = jnp.where(place == first + index, row, table)
    return table


def three_pieces(value):
    first = value.astype(jnp.bfloat16).astype(jnp.float32)
    rest = value - first
    second = rest.astype(jnp.bfloat16).astype(jnp.float32)
    return [first, second, rest - second]


def predict_kernel(
    channels, comps_ref, cells_ref, fractions_ref, observed_ref, counts_ref, weights_ref,
    residual_ref, packed_ref, left_ref,
):
    row_count = observed_ref.shape[0]
    comp_count = comps_ref.shape[0]
    tile_count, _, slot = packed_ref.shape
    row_block = min(128, row_count)
    comp_block = min(512, comp_count)

    factors = []
    for axis in range(2):
        cell = cells_ref[axis : axis + 1, :] + 3
        high = (cell + 32) >> 6
        low = (cell - 64 * high).astype(jnp.float32)
        high = jnp.where(high >= 64, high - 128, high)
        pieces = three_pieces(fractions_ref[axis : axis + 1, :])
        factors += [low, (64 * high).astype(jnp.float32)] + pieces + [low] + pieces
    table = place_rows((2 * channels, row_count), channels, factors) * (1.0 / GRID)
    left_ref[...] = table.T.astype(jnp.bfloat16)

    live = counts_ref[0, 0]
    for tile in range(1, tile_count):
        live = live + counts_ref[0, tile]

    @pl.loop(0, row_count // row_block)
    def _(step):
        start = pl.multiple_of(step * row_block, row_block)
        rows = pl.ds(start, row_block)
        left = left_ref[rows, :]
        real_part = jnp.zeros((row_block, 2 * channels), jnp.float32)
        imag_part = jnp.zeros((row_block, 2 * channels), jnp.float32)
        for first in range(0, comp_count, comp_block):
            comps = comps_ref[first : first + comp_block, :]
            turns = lax.dot_general(
                left, comps, (((1,), (1,)), ((), ())), preferred_element_type=jnp.float32
            )
            rest = turns - jnp.round(turns)
            square = rest * rest
            cosine = COS[-1] * square + COS[-2]
            for coefficient in COS[-3::-1]:
                cosine = cosine * square + coefficient
            sine = SIN[-1] * square + SIN[-2]
            for coefficient in SIN[-3::-1]:
                sine = sine * square + coefficient
            sine = sine * rest
            real_part += jnp.dot(
                cosine.astype(jnp.bfloat16), comps, preferred_element_type=jnp.float32
            )
            imag_part += jnp.dot(
                sine.astype(jnp.bfloat16), comps, preferred_element_type=jnp.float32
            )
        lane = lax.broadcasted_iota(jnp.int32, real_part.shape, 1)
        predicted = jnp.where(lane < channels, real_part, pltpu.roll(imag_part, channels, 1))
        row = start + lax.broadcasted_iota(jnp.int32, real_part.shape, 0)
        residual = jnp.where(row < live, observed_ref[rows, :].astype(jnp.float32) - predicted, 0.0)
        residual_ref[rows, :] = residual.astype(jnp.bfloat16)

    lane = lax.broadcasted_iota(jnp.int32, (1, 2 * channels), 1)
    weights = weights_ref[...]
    halves = [jnp.where(lane < channels, weights, 0.0), jnp.where(lane < channels, 0.0, weights)]
    weight_rows = [piece for half in halves for piece in three_pieces(half)]
    weight_table = place_rows((16, 2 * channels), 0, weight_rows).astype(jnp.bfloat16)
    sums = lax.dot_general(
        weight_table, residual_ref[...], (((1,), (1,)), ((), ())),
        preferred_element_type=jnp.float32,
    )
    data = place_rows(
        (8, row_count),
        0,
        [
            sums[0:1] + sums[1:2] + sums[2:3],
            sums[3:4] + sums[4:5] + sums[5:6],
            fractions_ref[0:1, :],
            fractions_ref[1:2, :],
            cells_ref[0:1, :].astype(jnp.float32),
            cells_ref[1:2, :].astype(jnp.float32),
        ],
    )
    begin = jnp.int32(0)
    place = lax.broadcasted_iota(jnp.int32, (8, slot), 0)
    index = lax.broadcasted_iota(jnp.int32, (8, slot), 1)
    for tile in range(tile_count):
        size = counts_ref[0, tile]
        moved = pltpu.roll(data, lax.rem(row_count - begin, row_count), 1)[:, :slot]
        packed_ref[tile] = jnp.where((place < 2) & (index >= size), 0.0, moved)
        begin = begin + size


def predict_rows(comps, cells, fractions, observed, bucket_counts, weights, slot):
    row_count, width = observed.shape
    tile_count = bucket_counts.shape[1]
    vmem = pl.BlockSpec(memory_space=pltpu.VMEM)
    return pl.pallas_call(
        functools.partial(predict_kernel, width // 2),
        out_shape=(
            jax.ShapeDtypeStruct(observed.shape, observed.dtype),
            jax.ShapeDtypeStruct((tile_count, 8, slot), jnp.float32),
        ),
        in_specs=[vmem, vmem, vmem, vmem, pl.BlockSpec(memory_space=pltpu.SMEM), vmem],
        out_specs=(vmem, vmem),
        scratch_shapes=[pltpu.VMEM((row_count, width), jnp.bfloat16)],
        compiler_params=pltpu.CompilerParams(vmem_limit_bytes=VMEM_LIMIT),
        name="predict_rows",
    )(comps, cells, fractions, observed, bucket_counts, weights)


def grid_kernel(
    n_vis, tile_width, data_ref, out_ref,
    rows_ref, left_ref, spread_ref, base_ref, sum_ref, own_ref, sent_ref, got_ref,
    send_sems, recv_sems,
):
    vis = lax.axis_index("vis")
    tile = lax.axis_index("tile")
    tile_count, _, slot = data_ref.shape
    owner_rows = sum_ref.shape[0] // n_vis
    chunk = sum_ref.shape[1]
    chunk_total = tile_width // chunk
    group = base_ref.shape[0]
    barrier = pltpu.get_barrier_semaphore()

    def peer(step):
        return {"vis": (vis + step) % n_vis}

    for step in range(1, n_vis):
        pl.semaphore_signal(barrier, inc=1, device_id=peer(step), device_id_type=MESH)

    for index in range(tile_count):
        rows_ref[:, index * slot : (index + 1) * slot] = data_ref[index]

    block = 2 * group
    for first in range(0, left_ref.shape[0], block):
        place = first + lax.broadcasted_iota(jnp.int32, (block, left_ref.shape[1]), 0)
        offset = (place >> 1).astype(jnp.float32) - 3.5 - rows_ref[5:6, :]
        shifted = offset - (rows_ref[3:4, :] - 0.5)
        weight = jnp.exp2(shifted * shifted * EXP_SCALE)
        value = jnp.where((place & 1) == 0, rows_ref[0:1, :], rows_ref[1:2, :])
        left_ref[first : first + block, :] = jnp.where(
            jnp.abs(offset) < 4.0, value * weight, 0.0
        ).astype(jnp.bfloat16)

    columns = rows_ref[4:5, :] - (tile * tile_width).astype(jnp.float32)
    lane_row = lax.broadcasted_iota(jnp.int32, base_ref.shape, 0).astype(jnp.float32)
    base_ref[...] = lane_row - 3.5 - columns

    def send(step, number):
        return pltpu.make_async_remote_copy(
            src_ref=sent_ref.at[(vis + step) % n_vis, number],
            dst_ref=got_ref.at[step, number],
            send_sem=send_sems.at[step, number],
            recv_sem=recv_sems.at[step, number],
            device_id=peer(step),
            device_id_type=MESH,
        )

    def compute(number):
        center = rows_ref[2:3, :] - 0.5
        start = number * chunk
        for first in range(0, chunk, group):
            offset = base_ref[...] + (start + first).astype(jnp.float32)
            shifted = offset - center
            weight = jnp.exp2(shifted * shifted * EXP_SCALE)
            spread_ref[first : first + group, :] = jnp.where(
                jnp.abs(offset) < 4.0, weight, 0.0
            ).astype(jnp.bfloat16)
        sum_ref[...] = lax.dot_general(
            left_ref[...], spread_ref[...], (((1,), (1,)), ((), ())),
            preferred_element_type=jnp.float32,
        )
        for owner in range(n_vis):
            sent_ref[owner, number] = sum_ref[
                owner * owner_rows : (owner + 1) * owner_rows, :
            ].astype(jnp.bfloat16)
        mine = pl.ds(pl.multiple_of(vis * owner_rows, owner_rows), owner_rows)
        own_ref[number] = sum_ref[mine, :]

    @pl.loop(0, chunk_total)
    def _(number):
        compute(number)

        @pl.when(number == 0)
        def _():
            pl.semaphore_wait(barrier, n_vis - 1)

        for step in range(1, n_vis):
            send(step, number).start()

    @pl.loop(0, chunk_total)
    def _(number):
        total = own_ref[number]
        for step in range(1, n_vis):
            send(step, number).wait_recv()
            total = total + got_ref[step, number].astype(jnp.float32)
        out_ref[:, pl.ds(pl.multiple_of(number * chunk, chunk), chunk)] = total

    @pl.loop(0, chunk_total)
    def _(number):
        for step in range(1, n_vis):
            send(step, number).wait_send()


def grid_rows(data, n_vis, tile_width):
    tile_count, _, slot = data.shape
    slots = tile_count * slot
    chunk = min(256, tile_width)
    chunk_total = tile_width // chunk
    owner_rows = 2 * BAND // n_vis
    vmem = pl.BlockSpec(memory_space=pltpu.VMEM)
    blocks = (n_vis, chunk_total, owner_rows, chunk)
    return pl.pallas_call(
        functools.partial(grid_kernel, n_vis, tile_width),
        out_shape=jax.ShapeDtypeStruct((owner_rows, tile_width), jnp.float32),
        in_specs=[vmem],
        out_specs=vmem,
        scratch_shapes=[
            pltpu.VMEM((8, slots), jnp.float32),
            pltpu.VMEM((2 * BAND, slots), jnp.bfloat16),
            pltpu.VMEM((chunk, slots), jnp.bfloat16),
            pltpu.VMEM((16, slots), jnp.float32),
            pltpu.VMEM((2 * BAND, chunk), jnp.float32),
            pltpu.VMEM((chunk_total, owner_rows, chunk), jnp.float32),
            pltpu.VMEM(blocks, jnp.bfloat16),
            pltpu.VMEM(blocks, jnp.bfloat16),
            pltpu.SemaphoreType.DMA((n_vis, chunk_total)),
            pltpu.SemaphoreType.DMA((n_vis, chunk_total)),
        ],
        compiler_params=pltpu.CompilerParams(
            collective_id=1, has_side_effects=True, vmem_limit_bytes=VMEM_LIMIT
        ),
        name="grid_rows",
    )(data)


def on_device(spectra, positions, observed, cells, fractions, bucket_counts, chan_weights):
    n_vis = lax.axis_size("vis")
    n_tile = lax.axis_size("tile")
    channels = chan_weights.shape[0]
    features = position_features(positions)
    spare = jnp.zeros((channels - features.shape[0], features.shape[1]), jnp.bfloat16)
    block = jnp.concatenate([spectra, features, spare], axis=0).T
    gathered = gather_components(block, n_vis, n_tile)
    comps = gathered.reshape(-1, 2 * channels)
    residual, packed = predict_rows(
        comps,
        cells,
        fractions,
        observed,
        bucket_counts,
        jnp.concatenate([chan_weights, chan_weights])[None, :],
        observed.shape[0] // 2,
    )
    packed = lax.all_to_all(packed, "tile", split_axis=0, concat_axis=0, tiled=True)
    share = grid_rows(packed, n_vis, GRID // n_tile)
    return (residual, share.reshape(BAND // n_vis, 2, GRID // n_tile))


def solution(mesh):
    placed = (
        P(None, ("vis", "tile")),
        P(None, ("vis", "tile")),
        P(("vis", "tile"), None),
        P(None, ("vis", "tile")),
        P(None, ("vis", "tile")),
        P(("vis", "tile"), None),
        P(),
    )
    return jax.shard_map(
        on_device,
        mesh=mesh,
        in_specs=placed,
        out_specs=(P(("vis", "tile"), None), P("vis", None, "tile")),
        check_vma=False,
    )
```

time: 340 us -> 75.2 us (0.22)
  waiting for transfers between devices: 100 us -> 0 us
  other arithmetic: 90.9 us -> 1.47 us
  blocking collectives: 81.3 us -> 8.08 us
  Pallas kernels: 0 us -> 59.5 us
  matrix products: 23.7 us -> 0 us
  local copies, waits for them, and re-layouts: 20.1 us -> 4.94 us
  between operations: 15 us -> 0.71 us
  starting transfers between devices: 7.56 us -> 0 us
    unnamed x2 -> x0, waiting for transfers between devices: 96.4 us -> none
    all_gather x2 -> x0, blocking collectives: 81.3 us -> none  [the longest x1 43.1 us: on_device(): lax.all_gather(positions, ('vis', 'tile'), axis=1, tiled=True)]
    dot_general x2 -> x0, other arithmetic: 70.5 us -> none  [the longest x1 35.4 us: predict_piece(): lax.dot_general(sine_table, spec_piece, contract_dims, preferred_element_...]
    pallas_call x0 -> x3, Pallas kernels: none -> 59.5 us  [the longest x1 31 us: grid_rows(): pl.pallas_call(functools.partial(grid_kernel, n_vis, tile_width), out_sha...]
    dot_general x10 -> x0, matrix products: 23.7 us -> none  [the longest x8 16.6 us: block_term(): jnp.einsum('cbv,bu->vcu', left_table, block_data[0], preferred_element_ty...]
    gather x4 -> x0, local copies, waits for them, and re-layouts: 11.6 us -> none  [the longest x2 5.8 us: on_device(): packed_cells = jnp.take(cell_rows, slot_index, axis=1).transpose(1, 0, 2)]
    convert_element_type x2 -> x0, other arithmetic: 11.4 us -> none  [the longest x1 11.3 us: spread_rows(): return place_taps(offset, kernel_weights(col_frac)).astype(jnp.bfloat16)]
    all_to_all x0 -> x1, blocking collectives: none -> 8.08 us  [on_device(): lax.all_to_all(packed, 'tile', split_axis=0, concat_axis=0, tiled=True)]
  transfers between devices with their start and end apart: 3 -> 0, of which waited for: 2 -> 0; matrix products, arithmetic and copies ran while one was open for 26% -> 0% of each run, Pallas kernels for 0% -> 0%
where the time goes in v1:
time: 75.2 us; the launch traced here: 74.7 us
  Pallas kernels  59.5 us (79%)
  blocking collectives  8.08 us (11%)
  local copies, waits for them, and re-layouts  4.94 us (7%)
  other arithmetic  1.47 us (2%)
    pallas_call x1, Pallas kernels, grid_rows(): pl.pallas_call(functools.partial(grid_kernel, n_vis, tile_width), out_sha...  31 us
    pallas_call x1, Pallas kernels, gather_components(): pl.pallas_call(functools.partial(gather_kernel, n_vis, n_tile), out_shape...  14.3 us
    pallas_call x1, Pallas kernels, predict_rows(): pl.pallas_call(functools.partial(predict_kernel, width // 2), out_shape=(...  14.2 us
    all_to_all x1, blocking collectives, on_device(): lax.all_to_all(packed, 'tile', split_axis=0, concat_axis=0, tiled=True)  8.08 us
    reshape x1, local copies, waits for them, and re-layouts, on_device(): return (residual, share.reshape(BAND // n_vis, 2, GRID // n_tile))  1.8 us

profile of v1, /device:TPU:0, one launch (start us, length us, event | category | flops | bytes accessed | tf_op | source)
XLA Modules:
  0.0 74.7 jit_solution(15014638097534130752)
XLA Ops:
  0.6 0.8 %fusion.1 = (bf16[1,64]{1,0:T(2,128)(2,1)S(1)}, s32[1,64]{1,0:T(1,128)S(1)}, bf16[1,64]{1,0:T(2,128)(2,1)S(1)}, s32[1,64]{1,0:T(1,128)S(1)}, s32[1,64]{1,0:T(1,128)S(1)}, /*index=5*/s32[1,64]{1,0:T(1,128)S(1)}) fusion(s32[2,64]{1,0:T(2,128)} %param.8), kind=kLoop, calls=%fused_computation.14 | loop fusion | flops 512 | bytes 1792 | tf_op jit(solution)/shard_map/convert.15
  1.4 0.1 copy.40
  1.5 0.0 copy-start.1
  1.5 0.1 copy.46
  1.6 0.6 copy-done.1
  2.2 0.6 maximum_bitcast_fusion.weights_ref
  2.8 0.1 copy.44
  2.9 0.1 copy.38
  3.0 0.0 copy-start
  3.1 0.1 copy.52
  3.2 0.1 copy.49
  3.3 0.5 copy-done
  3.8 0.1 copy.48
  3.9 0.1 copy.45
  4.0 0.1 copy.43
  4.0 0.1 copy.37
  4.1 0.1 copy.39
  4.2 0.1 copy.42
  4.3 0.1 copy.36
  4.5 0.8 %concatenate.7 = bf16[128,64]{0,1:T(8,128)(2,1)} concatenate(bf16[64,64]{0,1:T(8,128)(2,1)S(1)} %copy.48, bf16[1,64]{0,1:T(8,128)(2,1)S(1)} %subtract_convert_fusion.1, bf16[1,64]{0,1:T(8,128)(2,1)S(1)} %subtract_convert_fusion.1, bf16[1,64]{0,1:T(8,128)(2,1)S(1)} %subtract_convert_fusion.1, bf16[1,64]{0,1:T(8,128)(2,1)S(1)} %subtract_convert_fusion.1, ...), dimensions={0} | concatenate | bytes 32768 | tf_op jit(solution)/shard_map/concatenate | solution.py:370
  5.3 14.3 %gather_components.1 = bf16[2,16,64,128]{3,2,1,0:T(8,128)(2,1)} custom-call(bf16[64,128]{1,0:T(8,128)(2,1)} %bitcast.5), custom_call_target="tpu_custom_call" | custom-call | tf_op jit(solution)/shard_map/gather_components/pallas_call | solution.py:98
  19.6 14.2 %predict_rows.1 = (bf16[1024,128]{1,0:T(8,128)(2,1)}, f32[4,8,512]{2,1,0:T(8,128)}) custom-call(bf16[2048,128]{1,0:T(8,128)(2,1)} %bitcast.4, s32[2,1024]{1,0:T(2,128)} %cells_ref.1, f32[2,1024]{1,0:T(2,128)} %fractions_ref.1, bf16[1024,128]{1,0:T(8,128)(2,1)} %observed_ref.1, s32[1,4]{1,0:T(1,128)} %counts_ref.1, f32[1,128]{1,0:T(1,128)} %maximum_bitcast_fusion.weights_ref), custom_call_target="tpu_custom_call" | custom-call | tf_op jit(solution)/shard_map/predict_rows/pallas_call | solution.py:224
  33.8 8.1 %all_to_all.5.data_ref = f32[4,8,512]{2,1,0:T(8,128)} all-to-all(f32[4,8,512]{2,1,0:T(8,128)} %get-tuple-element.5), channel_id=1, replica_groups=mesh['vis'=8,'tile'=4] {'tile'}, dimensions={0} | all-to-all | bytes 131072 | tf_op jit(solution)/shard_map/all_to_all | solution.py:382
  41.9 31.0 %grid_rows.1 = f32[32,2048]{1,0:T(8,128)} custom-call(f32[4,8,512]{2,1,0:T(8,128)} %all_to_all.5.data_ref), custom_call_target="tpu_custom_call" | custom-call | tf_op jit(solution)/shard_map/grid_rows/pallas_call | solution.py:340
  72.9 1.8 %reshape.11 = f32[16,2,2048]{2,1,0:T(2,128)} reshape(f32[32,2048]{1,0:T(8,128)} %grid_rows.1) | data formatting | bytes 524288 | tf_op jit(solution)/shard_map/reshape | solution.py:384
  (7 shorter events, 0.1 us)
Async XLA Ops:
  1.5 0.7 copy-start.1
  3.0 0.7 copy-start

commit v2 on v1

--- a/solution.py
+++ b/solution.py
@@ -13,6 +13,7 @@
 TAPS = 8
 MESH = pl.DeviceIdType.MESH
 VMEM_LIMIT = 60 * 1024 * 1024
+LAG = 2
 
 COS = (0.9999992107823198, -19.73898035576402, 64.92865742103395, -85.2716215343041,
        58.79049212014272, -21.071105627647917)
@@ -237,22 +238,28 @@
 
 def grid_kernel(
     n_vis, tile_width, data_ref, out_ref,
-    rows_ref, left_ref, spread_ref, base_ref, sum_ref, own_ref, sent_ref, got_ref,
-    send_sems, recv_sems,
+    rows_ref, left_ref, spread_ref, base_ref, sum_ref, keep_ref, own_ref,
+    pair_sent_ref, pair_got_ref, sent_ref, got_ref,
+    pair_send_sems, pair_recv_sems, send_sems, recv_sems,
 ):
     vis = lax.axis_index("vis")
     tile = lax.axis_index("tile")
     tile_count, _, slot = data_ref.shape
-    owner_rows = sum_ref.shape[0] // n_vis
-    chunk = sum_ref.shape[1]
+    half = n_vis // 2
+    owner_rows = own_ref.shape[1]
+    chunk = own_ref.shape[2]
     chunk_total = tile_width // chunk
     group = base_ref.shape[0]
+    side = vis % 2
+    mine = vis // 2
+    partner = {"vis": vis + 1 - 2 * side}
     barrier = pltpu.get_barrier_semaphore()
 
     def peer(step):
-        return {"vis": (vis + step) % n_vis}
-
-    for step in range(1, n_vis):
+        return {"vis": ((mine + step) % half) * 2 + side}
+
+    pl.semaphore_signal(barrier, inc=1, device_id=partner, device_id_type=MESH)
+    for step in range(1, half):
         pl.semaphore_signal(barrier, inc=1, device_id=peer(step), device_id_type=MESH)
 
     for index in range(tile_count):
@@ -273,9 +280,19 @@
     lane_row = lax.broadcasted_iota(jnp.int32, base_ref.shape, 0).astype(jnp.float32)
     base_ref[...] = lane_row - 3.5 - columns
 
+    def pair_send(number):
+        return pltpu.make_async_remote_copy(
+            src_ref=pair_sent_ref.at[number],
+            dst_ref=pair_got_ref.at[number],
+            send_sem=pair_send_sems.at[number],
+            recv_sem=pair_recv_sems.at[number],
+            device_id=partner,
+            device_id_type=MESH,
+        )
+
     def send(step, number):
         return pltpu.make_async_remote_copy(
-            src_ref=sent_ref.at[(vis + step) % n_vis, number],
+            src_ref=sent_ref.at[step, number],
             dst_ref=got_ref.at[step, number],
             send_sem=send_sems.at[step, number],
             recv_sem=recv_sems.at[step, number],
@@ -293,16 +310,24 @@
             spread_ref[first : first + group, :] = jnp.where(
                 jnp.abs(offset) < 4.0, weight, 0.0
             ).astype(jnp.bfloat16)
-        sum_ref[...] = lax.dot_general(
+        sums = lax.dot_general(
             left_ref[...], spread_ref[...], (((1,), (1,)), ((), ())),
             preferred_element_type=jnp.float32,
         )
-        for owner in range(n_vis):
-            sent_ref[owner, number] = sum_ref[
-                owner * owner_rows : (owner + 1) * owner_rows, :
-            ].astype(jnp.bfloat16)
-        mine = pl.ds(pl.multiple_of(vis * owner_rows, owner_rows), owner_rows)
-        own_ref[number] = sum_ref[mine, :]
+        sum_ref[...] = sums.reshape(sum_ref.shape)
+        for place in range(half):
+            pair_sent_ref[number, place] = sum_ref[2 * place + 1 - side].astype(jnp.bfloat16)
+            keep_ref[number, place] = sum_ref[2 * place + side]
+
+    def combine(number):
+        pair_send(number).wait_recv()
+        own_ref[number] = keep_ref[number, mine] + pair_got_ref[number, mine].astype(jnp.float32)
+        for step in range(1, half):
+            place = (mine + step) % half
+            total = keep_ref[number, place] + pair_got_ref[number, place].astype(jnp.float32)
+            sent_ref[step, number] = total.astype(jnp.bfloat16)
+        for step in range(1, half):
+            send(step, number).start()
 
     @pl.loop(0, chunk_total)
     def _(number):
@@ -310,22 +335,30 @@
 
         @pl.when(number == 0)
         def _():
-            pl.semaphore_wait(barrier, n_vis - 1)
-
-        for step in range(1, n_vis):
-            send(step, number).start()
+            pl.semaphore_wait(barrier, half)
+
+        pair_send(number).start()
+
+        @pl.when(number >= LAG)
+        def _():
+            combine(number - LAG)
+
+    @pl.loop(max(chunk_total - LAG, 0), chunk_total)
+    def _(number):
+        combine(number)
 
     @pl.loop(0, chunk_total)
     def _(number):
         total = own_ref[number]
-        for step in range(1, n_vis):
+        for step in range(1, half):
             send(step, number).wait_recv()
             total = total + got_ref[step, number].astype(jnp.float32)
         out_ref[:, pl.ds(pl.multiple_of(number * chunk, chunk), chunk)] = total
 
     @pl.loop(0, chunk_total)
     def _(number):
-        for step in range(1, n_vis):
+        pair_send(number).wait_send()
+        for step in range(1, half):
             send(step, number).wait_send()
 
 
@@ -335,8 +368,10 @@
     chunk = min(256, tile_width)
     chunk_total = tile_width // chunk
     owner_rows = 2 * BAND // n_vis
+    half = n_vis // 2
     vmem = pl.BlockSpec(memory_space=pltpu.VMEM)
-    blocks = (n_vis, chunk_total, owner_rows, chunk)
+    pair_blocks = (chunk_total, half, owner_rows, chunk)
+    blocks = (half, chunk_total, owner_rows, chunk)
     return pl.pallas_call(
         functools.partial(grid_kernel, n_vis, tile_width),
         out_shape=jax.ShapeDtypeStruct((owner_rows, tile_width), jnp.float32),
@@ -347,12 +382,17 @@
             pltpu.VMEM((2 * BAND, slots), jnp.bfloat16),
             pltpu.VMEM((chunk, slots), jnp.bfloat16),
             pltpu.VMEM((16, slots), jnp.float32),
-            pltpu.VMEM((2 * BAND, chunk), jnp.float32),
+            pltpu.VMEM((n_vis, owner_rows, chunk), jnp.float32),
+            pltpu.VMEM(pair_blocks, jnp.float32),
             pltpu.VMEM((chunk_total, owner_rows, chunk), jnp.float32),
+            pltpu.VMEM(pair_blocks, jnp.bfloat16),
+            pltpu.VMEM(pair_blocks, jnp.bfloat16),
             pltpu.VMEM(blocks, jnp.bfloat16),
             pltpu.VMEM(blocks, jnp.bfloat16),
-            pltpu.SemaphoreType.DMA((n_vis, chunk_total)),
-            pltpu.SemaphoreType.DMA((n_vis, chunk_total)),
+            pltpu.SemaphoreType.DMA((chunk_total,)),
+            pltpu.SemaphoreType.DMA((chunk_total,)),
+            pltpu.SemaphoreType.DMA((half, chunk_total)),
+            pltpu.SemaphoreType.DMA((half, chunk_total)),
         ],
         compiler_params=pltpu.CompilerParams(
             collective_id=1, has_side_effects=True, vmem_limit_bytes=VMEM_LIMIT

time: 75.2 us -> 69.2 us (0.920)
  Pallas kernels: 59.5 us -> 53.5 us
    pallas_call x1, Pallas kernels: 31 us -> 25 us  [grid_rows(): pl.pallas_call(functools.partial(grid_kernel, n_vis, tile_width), out_sha...]
where the time goes in v2:
time: 69.2 us; the launch traced here: 68.7 us
  Pallas kernels  53.5 us (77%)
  blocking collectives  8.08 us (12%)
  local copies, waits for them, and re-layouts  4.94 us (7%)
  other arithmetic  1.47 us (2%)
  between operations  0.71 us (1%)
    pallas_call x1, Pallas kernels, grid_rows(): pl.pallas_call(functools.partial(grid_kernel, n_vis, tile_width), out_sha...  25 us
    pallas_call x1, Pallas kernels, gather_components(): pl.pallas_call(functools.partial(gather_kernel, n_vis, n_tile), out_shape...  14.3 us
    pallas_call x1, Pallas kernels, predict_rows(): pl.pallas_call(functools.partial(predict_kernel, width // 2), out_shape=(...  14.2 us
    all_to_all x1, blocking collectives, on_device(): lax.all_to_all(packed, 'tile', split_axis=0, concat_axis=0, tiled=True)  8.08 us
    reshape x1, local copies, waits for them, and re-layouts, on_device(): return (residual, share.reshape(BAND // n_vis, 2, GRID // n_tile))  1.8 us

profile of v2, /device:TPU:0, one launch (start us, length us, event | category | flops | bytes accessed | tf_op | source)
XLA Modules:
  0.0 68.7 jit_solution(884130574786760932)
XLA Ops:
  0.6 0.8 %fusion.1 = (bf16[1,64]{1,0:T(2,128)(2,1)S(1)}, s32[1,64]{1,0:T(1,128)S(1)}, bf16[1,64]{1,0:T(2,128)(2,1)S(1)}, s32[1,64]{1,0:T(1,128)S(1)}, s32[1,64]{1,0:T(1,128)S(1)}, /*index=5*/s32[1,64]{1,0:T(1,128)S(1)}) fusion(s32[2,64]{1,0:T(2,128)} %param.8), kind=kLoop, calls=%fused_computation.14 | loop fusion | flops 512 | bytes 1792 | tf_op jit(solution)/shard_map/convert.15
  1.4 0.1 copy.40
  1.5 0.0 copy-start.1
  1.5 0.1 copy.46
  1.6 0.6 copy-done.1
  2.2 0.6 maximum_bitcast_fusion.weights_ref
  2.8 0.1 copy.44
  2.9 0.1 copy.38
  3.0 0.0 copy-start
  3.1 0.1 copy.52
  3.2 0.1 copy.49
  3.3 0.5 copy-done
  3.8 0.1 copy.48
  3.9 0.1 copy.45
  4.0 0.1 copy.43
  4.0 0.1 copy.37
  4.1 0.1 copy.39
  4.2 0.1 copy.42
  4.3 0.1 copy.36
  4.5 0.8 %concatenate.7 = bf16[128,64]{0,1:T(8,128)(2,1)} concatenate(bf16[64,64]{0,1:T(8,128)(2,1)S(1)} %copy.48, bf16[1,64]{0,1:T(8,128)(2,1)S(1)} %subtract_convert_fusion.1, bf16[1,64]{0,1:T(8,128)(2,1)S(1)} %subtract_convert_fusion.1, bf16[1,64]{0,1:T(8,128)(2,1)S(1)} %subtract_convert_fusion.1, bf16[1,64]{0,1:T(8,128)(2,1)S(1)} %subtract_convert_fusion.1, ...), dimensions={0} | concatenate | bytes 32768 | tf_op jit(solution)/shard_map/concatenate | solution.py:410
  5.3 14.3 %gather_components.1 = bf16[2,16,64,128]{3,2,1,0:T(8,128)(2,1)} custom-call(bf16[64,128]{1,0:T(8,128)(2,1)} %bitcast.5), custom_call_target="tpu_custom_call" | custom-call | tf_op jit(solution)/shard_map/gather_components/pallas_call | solution.py:99
  19.6 14.2 %predict_rows.1 = (bf16[1024,128]{1,0:T(8,128)(2,1)}, f32[4,8,512]{2,1,0:T(8,128)}) custom-call(bf16[2048,128]{1,0:T(8,128)(2,1)} %bitcast.4, s32[2,1024]{1,0:T(2,128)} %cells_ref.1, f32[2,1024]{1,0:T(2,128)} %fractions_ref.1, bf16[1024,128]{1,0:T(8,128)(2,1)} %observed_ref.1, s32[1,4]{1,0:T(1,128)} %counts_ref.1, f32[1,128]{1,0:T(1,128)} %maximum_bitcast_fusion.weights_ref), custom_call_target="tpu_custom_call" | custom-call | tf_op jit(solution)/shard_map/predict_rows/pallas_call | solution.py:225
  33.8 8.1 %all_to_all.5.data_ref = f32[4,8,512]{2,1,0:T(8,128)} all-to-all(f32[4,8,512]{2,1,0:T(8,128)} %get-tuple-element.5), channel_id=1, replica_groups=mesh['vis'=8,'tile'=4] {'tile'}, dimensions={0} | all-to-all | bytes 131072 | tf_op jit(solution)/shard_map/all_to_all | solution.py:422
  41.9 25.0 %grid_rows.1 = f32[32,2048]{1,0:T(8,128)} custom-call(f32[4,8,512]{2,1,0:T(8,128)} %all_to_all.5.data_ref), custom_call_target="tpu_custom_call" | custom-call | tf_op jit(solution)/shard_map/grid_rows/pallas_call | solution.py:375
  66.9 1.8 %reshape.11 = f32[16,2,2048]{2,1,0:T(2,128)} reshape(f32[32,2048]{1,0:T(8,128)} %grid_rows.1) | data formatting | bytes 524288 | tf_op jit(solution)/shard_map/reshape | solution.py:424
  (7 shorter events, 0.1 us)
Async XLA Ops:
  1.5 0.7 copy-start.1
  3.0 0.7 %copy-start = (bf16[64,64]{1,0:T(8,128)(2,1)S(1)}, bf16[64,64]{1,0:T(8,128)(2,1)}, u32[]{:S(2)}) copy-start(bf16[64,64]{1,0:T(8,128)(2,1)} %param.7) | copy-start | bytes 24580

commit v3 on v2

--- a/solution.py
+++ b/solution.py
@@ -241,6 +241,7 @@
     rows_ref, left_ref, spread_ref, base_ref, sum_ref, keep_ref, own_ref,
     pair_sent_ref, pair_got_ref, sent_ref, got_ref,
     pair_send_sems, pair_recv_sems, send_sems, recv_sems,
+    slots_ref, slot_send_sems, slot_recv_sems,
 ):
     vis = lax.axis_index("vis")
     tile = lax.axis_index("tile")
@@ -262,8 +263,30 @@
     for step in range(1, half):
         pl.semaphore_signal(barrier, inc=1, device_id=peer(step), device_id_type=MESH)
 
-    for index in range(tile_count):
-        rows_ref[:, index * slot : (index + 1) * slot] = data_ref[index]
+    def owner(step):
+        return (tile + step) % tile_count
+
+    def slot_send(step):
+        return pltpu.make_async_remote_copy(
+            src_ref=data_ref.at[owner(step)],
+            dst_ref=slots_ref.at[step],
+            send_sem=slot_send_sems.at[step],
+            recv_sem=slot_recv_sems.at[step],
+            device_id={"tile": owner(step)},
+            device_id_type=MESH,
+        )
+
+    for step in range(1, tile_count):
+        pl.semaphore_signal(
+            barrier, inc=1, device_id={"tile": owner(step)}, device_id_type=MESH
+        )
+    pl.semaphore_wait(barrier, half + tile_count - 1)
+    for step in range(1, tile_count):
+        slot_send(step).start()
+    rows_ref[:, :slot] = data_ref[tile]
+    for step in range(1, tile_count):
+        slot_send(step).wait_recv()
+        rows_ref[:, step * slot : (step + 1) * slot] = slots_ref[step]
 
     block = 2 * group
     for first in range(0, left_ref.shape[0], block):
@@ -333,10 +356,6 @@
     def _(number):
         compute(number)
 
-        @pl.when(number == 0)
-        def _():
-            pl.semaphore_wait(barrier, half)
-
         pair_send(number).start()
 
         @pl.when(number >= LAG)
@@ -354,6 +373,9 @@
             send(step, number).wait_recv()
             total = total + got_ref[step, number].astype(jnp.float32)
         out_ref[:, pl.ds(pl.multiple_of(number * chunk, chunk), chunk)] = total
+
+    for step in range(1, tile_count):
+        slot_send(step).wait_send()
 
     @pl.loop(0, chunk_total)
     def _(number):
@@ -393,6 +415,9 @@
             pltpu.SemaphoreType.DMA((chunk_total,)),
             pltpu.SemaphoreType.DMA((half, chunk_total)),
             pltpu.SemaphoreType.DMA((half, chunk_total)),
+            pltpu.VMEM(data.shape, jnp.float32),
+            pltpu.SemaphoreType.DMA((tile_count,)),
+            pltpu.SemaphoreType.DMA((tile_count,)),
         ],
         compiler_params=pltpu.CompilerParams(
             collective_id=1, has_side_effects=True, vmem_limit_bytes=VMEM_LIMIT
@@ -419,7 +444,6 @@
         jnp.concatenate([chan_weights, chan_weights])[None, :],
         observed.shape[0] // 2,
     )
-    packed = lax.all_to_all(packed, "tile", split_axis=0, concat_axis=0, tiled=True)
     share = grid_rows(packed, n_vis, GRID // n_tile)
     return (residual, share.reshape(BAND // n_vis, 2, GRID // n_tile))
 

time: 69.2 us -> 64.8 us (0.936)
  blocking collectives: 8.08 us -> 0 us
  Pallas kernels: 53.5 us -> 57.9 us
    all_to_all x1 -> x0, blocking collectives: 8.08 us -> none  [on_device(): lax.all_to_all(packed, 'tile', split_axis=0, concat_axis=0, tiled=True)]
    pallas_call x1, Pallas kernels: 25 us -> 29.4 us  [grid_rows(): pl.pallas_call(functools.partial(grid_kernel, n_vis, tile_width), out_sha...]
    another operation x5, other arithmetic: 0.81 us -> 0.06 us
    broadcast_in_dim x1, other arithmetic: 0.65 us -> 1.38 us  [on_device(): jnp.concatenate([chan_weights, chan_weights])[None, :]]
where the time goes in v3:
time: 64.8 us; the launch traced here: 64.5 us
  Pallas kernels  57.9 us (89%)
  local copies, waits for them, and re-layouts  4.38 us (7%)
  other arithmetic  1.45 us (2%)
  between operations  0.71 us (1%)
    pallas_call x1, Pallas kernels, grid_rows(): pl.pallas_call(functools.partial(grid_kernel, n_vis, tile_width), out_sha...  29.4 us
    pallas_call x1, Pallas kernels, gather_components(): pl.pallas_call(functools.partial(gather_kernel, n_vis, n_tile), out_shape...  14.3 us
    pallas_call x1, Pallas kernels, predict_rows(): pl.pallas_call(functools.partial(predict_kernel, width // 2), out_shape=(...  14.2 us
    reshape x1, local copies, waits for them, and re-layouts, on_device(): return (residual, share.reshape(BAND // n_vis, 2, GRID // n_tile))  1.8 us
    broadcast_in_dim x1, other arithmetic, on_device(): jnp.concatenate([chan_weights, chan_weights])[None, :]  1.38 us

profile of v3, /device:TPU:0, one launch (start us, length us, event | category | flops | bytes accessed | tf_op | source)
XLA Modules:
  0.0 64.5 jit_solution(14216792619466502499)
XLA Ops:
  0.6 0.0 copy-start.1
  0.6 1.4 %maximum_bitcast_fusion.weights_ref = f32[1,128]{1,0:T(1,128)} fusion(f32[64]{0:T(128)} %param.13), kind=kLoop, calls=%fused_computation.4 | loop fusion | flops 128 | bytes 768 | tf_op jit(solution)/shard_map/broadcast_in_dim | solution.py:444
  2.0 0.0 copy-done.1
  2.1 0.1 copy.44
  2.2 0.1 copy.38
  2.3 0.0 copy-start
  2.3 0.1 copy.52
  2.4 0.1 copy.49
  2.5 0.5 copy-done
  3.0 0.1 copy.48
  3.1 0.1 copy.45
  3.2 0.1 copy.40
  3.3 0.1 copy.46
  3.4 0.1 copy.43
  3.5 0.1 copy.37
  3.6 0.1 copy.39
  3.7 0.1 copy.42
  3.8 0.1 copy.36
  4.0 0.8 %concatenate.7 = bf16[128,64]{0,1:T(8,128)(2,1)} concatenate(bf16[64,64]{0,1:T(8,128)(2,1)S(1)} %copy.48, bf16[1,64]{0,1:T(8,128)(2,1)S(1)} %subtract_convert_fusion.1, bf16[1,64]{0,1:T(8,128)(2,1)S(1)} %subtract_convert_fusion.1, bf16[1,64]{0,1:T(8,128)(2,1)S(1)} %subtract_convert_fusion.1, bf16[1,64]{0,1:T(8,128)(2,1)S(1)} %subtract_convert_fusion.1, ...), dimensions={0} | concatenate | bytes 32768 | tf_op jit(solution)/shard_map/concatenate | solution.py:435
  4.7 14.3 %gather_components.1 = bf16[2,16,64,128]{3,2,1,0:T(8,128)(2,1)} custom-call(bf16[64,128]{1,0:T(8,128)(2,1)} %bitcast.5), custom_call_target="tpu_custom_call" | custom-call | tf_op jit(solution)/shard_map/gather_components/pallas_call | solution.py:99
  19.0 14.2 %predict_rows.1 = (bf16[1024,128]{1,0:T(8,128)(2,1)}, f32[4,8,512]{2,1,0:T(8,128)}) custom-call(bf16[2048,128]{1,0:T(8,128)(2,1)} %bitcast.4, s32[2,1024]{1,0:T(2,128)} %cells_ref.1, f32[2,1024]{1,0:T(2,128)} %fractions_ref.1, bf16[1024,128]{1,0:T(8,128)(2,1)} %observed_ref.1, s32[1,4]{1,0:T(1,128)} %counts_ref.1, f32[1,128]{1,0:T(1,128)} %maximum_bitcast_fusion.weights_ref), custom_call_target="tpu_custom_call" | custom-call | tf_op jit(solution)/shard_map/predict_rows/pallas_call | solution.py:225
  33.3 29.4 %grid_rows.1 = f32[32,2048]{1,0:T(8,128)} custom-call(f32[4,8,512]{2,1,0:T(8,128)} %get-tuple-element.5.data_ref), custom_call_target="tpu_custom_call" | custom-call | tf_op jit(solution)/shard_map/grid_rows/pallas_call | solution.py:397
  62.7 1.8 %reshape.11 = f32[16,2,2048]{2,1,0:T(2,128)} reshape(f32[32,2048]{1,0:T(8,128)} %grid_rows.1) | data formatting | bytes 524288 | tf_op jit(solution)/shard_map/reshape | solution.py:448
  (8 shorter events, 0.1 us)
Async XLA Ops:
  0.6 1.4 %copy-start.1 = (s32[2,64]{1,0:T(2,128)S(1)}, s32[2,64]{1,0:T(2,128)}, u32[]{:S(2)}) copy-start(s32[2,64]{1,0:T(2,128)} %param.8) | copy-start | bytes 1540
  2.3 0.7 %copy-start = (bf16[64,64]{1,0:T(8,128)(2,1)S(1)}, bf16[64,64]{1,0:T(8,128)(2,1)}, u32[]{:S(2)}) copy-start(bf16[64,64]{1,0:T(8,128)(2,1)} %param.7) | copy-start | bytes 24580
